TPU v7x, 32 devices: a whole 2x2x4 slice. The times are simulated.
32 devices in a mesh: rows: 8 (over z, y), rep: 4 (over x, core).
Axes of the slice: x: 2, y: 2, z: 4, core: 2. Of those that a mesh axis runs over, the one named last changes fastest.
Arguments:
- field_in: bfloat16 [64, 384, 256], P('rows'), may hold values from -6 to 6
- left_factors: bfloat16 [1024, 384, 64], P(('rows', 'rep')), may hold values from -0.3125 to 0.3125
- right_factors: bfloat16 [1024, 384, 64], P(('rows', 'rep')), may hold values from -0.1875 to 0.1875
- block_ranks: int32 [1024], P(('rows', 'rep')), may hold values from 8 to 64
- row_cluster: int32 [1024], P(('rows', 'rep')), may hold values from 0 to 7
- col_owner: int32 [1024, 1], P(('rows', 'rep')), may hold values from 0 to 7; in each aligned block of 32 rows (0 to 31, 32 to 63, ...) at most 6 rows name the same one
- col_cluster: int32 [1024], P(('rows', 'rep')), may hold values from 0 to 7
- near_blocks: bfloat16 [64, 3, 384, 384], P('rows', None, 'rep'), may hold values from -0.1875 to 0.1875
Outputs:
- result_field: float32 [64, 384, 256], P('rows')
Inputs may be any that keep to these rules, and one draw needn't show every extreme that they name: `col_owner`: among the 32 blocks of one device no owner is named more than once.
All inputs are finite; a program needn't handle non-finite values.
Results may differ from a plain program's by a relative error of at most 0.0029.
Values may be sent and summed in bfloat16 or wider, within the bound.
A program may use at most 128 MiB of HBM per device.

v0:
```python
import jax
import jax.numpy as jnp
from jax import lax
from jax.sharding import PartitionSpec as P


def from_behind(value, axis, steps):
    count = lax.axis_size(axis)
    pairs = [(source, (source + steps) % count) for source in range(count)]
    return lax.ppermute(value, axis, pairs)


def shards(
    field_in,
    left_factors,
    right_factors,
    block_ranks,
    row_cluster,
    col_owner,
    col_cluster,
    near_blocks,
):
    owners = lax.axis_size("rows")
    blocks, width, rank_pad = left_factors.shape
    clusters, _, columns = field_in.shape
    most_slots = 5 * blocks // (4 * owners) + 1
    slot_count = owners * most_slots
    picked = jnp.take(field_in, row_cluster, axis=0)
    coeffs = jnp.einsum("bcr,bcn->brn", left_factors, picked, preferred_element_type=jnp.float32)
    keeper = jnp.arange(rank_pad, dtype=jnp.int32)[None, :, None] < block_ranks[:, None, None]
    coeffs = jnp.where(keeper, coeffs, jnp.float32(0.0)).astype(jnp.bfloat16)
    target = col_owner[:, 0]
    owner_hits = (target[:, None] == jnp.arange(owners, dtype=jnp.int32)[None, :]).astype(jnp.int32)
    earlier = jnp.sum((jnp.cumsum(owner_hits, axis=0) - 1) * owner_hits, axis=1)
    slot_index = target * most_slots + earlier
    labels = jnp.full((slot_count,), clusters, jnp.int32).at[slot_index].set(col_cluster)
    arrived = lax.all_to_all(
        labels.reshape(owners, most_slots), "rows", split_axis=0, concat_axis=0, tiled=True
    )
    packed_right = (
        jnp.zeros((slot_count, width, rank_pad), jnp.bfloat16).at[slot_index].set(right_factors)
    )
    packed_coeffs = (
        jnp.zeros((slot_count, rank_pad, columns), jnp.bfloat16).at[slot_index].set(coeffs)
    )
    received = jnp.einsum(
        "smcr,smrn->smcn",
        lax.all_to_all(
            packed_right.reshape(owners, most_slots, width, rank_pad),
            "rows",
            split_axis=0,
            concat_axis=0,
            tiled=True,
        ),
        lax.all_to_all(
            packed_coeffs.reshape(owners, most_slots, rank_pad, columns),
            "rows",
            split_axis=0,
            concat_axis=0,
            tiled=True,
        ),
        preferred_element_type=jnp.float32,
    ).astype(jnp.bfloat16)
    flattened = received.reshape(slot_count, width * columns)
    chooser = (
        jnp.arange(clusters, dtype=jnp.int32)[:, None] == arrived.reshape(slot_count)[None, :]
    ).astype(jnp.bfloat16)
    far_field = jnp.dot(chooser, flattened, preferred_element_type=jnp.float32).reshape(
        clusters, width, columns
    )
    share = near_blocks.shape[2]
    offset_rows = lax.axis_index("rep") * share
    local_rows = lax.dynamic_slice_in_dim(field_in, offset_rows, share, 1)
    terms = [
        jnp.einsum(
            "cpq,cpn->cqn", near_blocks[:, offset], local_rows, preferred_element_type=jnp.float32
        )
        for offset in range(3)
    ]
    from_prev = from_behind(terms[2][-1:], "rows", 1)
    from_next = from_behind(terms[0][:1], "rows", -1)
    total_here = (
        far_field
        + terms[1]
        + jnp.concatenate([from_prev, terms[2][:-1]], axis=0)
        + jnp.concatenate([terms[0][1:], from_next], axis=0)
    )
    return lax.psum(total_here, "rep")


def solution(mesh):
    in_specs = (
        P("rows", None, None),
        P(("rows", "rep"), None, None),
        P(("rows", "rep"), None, None),
        P(("rows", "rep")),
        P(("rows", "rep")),
        P(("rows", "rep"), None),
        P(("rows", "rep")),
        P("rows", None, "rep", None),
    )
    out_specs = P("rows", None, None)
    return jax.shard_map(shards, mesh=mesh, in_specs=in_specs, out_specs=out_specs, check_vma=False)
```

profile of v0, /device:TPU:0, one launch (start us, length us, event | category | flops | bytes accessed | tf_op | source)
XLA Modules:
  0.0 235.9 jit_solution(18251465345047617416)
XLA Ops:
  6.5 0.8 fusion.27
  7.4 0.8 select_reduce_fusion
  8.3 0.7 fusion.31
  8.9 0.8 scatter_custom_fusion
  9.8 0.7 all_to_all.12
  10.4 7.3 %all-to-all-start = ((s32[8,1,6]{2,1,0:T(1,128)}), s32[8,1,6]{2,1,0:T(1,128)S(1)}, u32[]{:S(2)}, u32[]{:S(2)}) async-start(s32[8,1,6]{2,1,0:T(1,128)} %bitcast.3), calls=%async_computation | async-start | bytes 8192 | tf_op jit(solution)/shard_map/all_to_all | solution.py:37
  19.1 0.7 iota_compare_fusion
  19.8 3.6 %gather_fusion = bf16[32,384,256]{2,1,0:T(8,128)(2,1)} fusion(bf16[8,384,256]{2,1,0:T(8,128)(2,1)S(1)} %copy-done, s32[1024]{0:T(1024)S(1)} %pad_clamp_fusion), kind=kCustom, calls=%fused_computation | custom fusion | bytes 12583040 | tf_op jit(solution)/shard_map/jit(_take)/gather | solution.py:28
  23.4 4.9 %fusion.12 = bf16[32,64,256]{2,1,0:T(8,128)(2,1)S(1)} fusion(bf16[32,384,64]{1,2,0:T(8,128)(2,1)} %param.9, bf16[32,384,256]{2,1,0:T(8,128)(2,1)} %gather_fusion, pred[32]{0:T(512)(128)(4,1)S(1)} %compare_and_fusion, pred[32,64]{1,0:T(8,128)(4,1)S(1)} %iota_compare_fusion), kind=kOutput, calls=%fused_computation.16 | convolution fusion | flops 406847488 | bytes 8914976 | tf_op jit(solution)/shard_map/bcr,bcn->brn/dot_general | solution.py:29
  28.3 1.3 broadcast_in_dim.42
  29.7 4.6 %scatter_fusion.1 = bf16[48,64,256]{2,1,0:T(8,128)(2,1)} fusion(bf16[48,64,256]{2,1,0:T(8,128)(2,1)} %broadcast_in_dim.42, s32[32]{0:T(128)S(1)} %fusion.31, bf16[32,64,256]{2,1,0:T(8,128)(2,1)S(1)} %fusion.12), kind=kCustom, calls=%fused_computation.3 | custom fusion | bytes 3145856 | tf_op jit(solution)/shard_map/scatter | solution.py:44
  34.2 6.0 %all-to-all-start.2 = ((bf16[8,6,64,256]{3,2,1,0:T(8,128)(2,1)}), bf16[8,6,64,256]{3,2,1,0:T(8,128)(2,1)S(1)}, u32[]{:S(2)}, u32[]{:S(2)}) async-start(bf16[8,6,64,256]{3,2,1,0:T(8,128)(2,1)} %bitcast.7), calls=%async_computation.2 | async-start | bytes 3145728 | tf_op jit(solution)/shard_map/all_to_all | solution.py:55
  40.2 1.9 broadcast_in_dim.41
  42.1 5.8 %scatter_fusion = bf16[48,384,64]{1,2,0:T(8,128)(2,1)} fusion(bf16[48,384,64]{1,2,0:T(8,128)(2,1)} %broadcast_in_dim.41, s32[32]{0:T(128)S(1)} %fusion.31, bf16[32,384,64]{1,2,0:T(8,128)(2,1)} %param.10), kind=kCustom, calls=%fused_computation.2 | custom fusion | bytes 4718720 | tf_op jit(solution)/shard_map/scatter | solution.py:41
  47.9 28.8 %all-to-all-done.2 = bf16[8,6,64,256]{3,2,1,0:T(8,128)(2,1)S(1)} async-done(((bf16[8,6,64,256]{3,2,1,0:T(8,128)(2,1)}), bf16[8,6,64,256]{3,2,1,0:T(8,128)(2,1)S(1)}, u32[]{:S(2)}, u32[]{:S(2)}) %all-to-all-start.2) | async-done | bytes 1572896 | tf_op jit(solution)/shard_map/all_to_all | solution.py:55
  76.7 4.4 %all-to-all-start.1 = ((bf16[8,6,384,64]{2,3,1,0:T(8,128)(2,1)}), bf16[8,6,384,64]{2,3,1,0:T(8,128)(2,1)}, u32[]{:S(2)}, u32[]{:S(2)}) async-start(bf16[8,6,384,64]{2,3,1,0:T(8,128)(2,1)} %bitcast.55), calls=%async_computation.1 | async-start | bytes 4718592 | tf_op jit(solution)/shard_map/all_to_all | solution.py:48
  81.1 3.4 %fusion.17 = f32[8,256,384]{2,1,0:T(8,128)} fusion(bf16[8,3,96,384]{3,2,1,0:T(8,128)(2,1)} %param.15, bf16[8,384,256]{2,1,0:T(8,128)(2,1)S(1)} %copy-done, s32[]{:T(128)S(6)} %select_n.27), kind=kOutput, calls=%fused_computation.19 | convolution fusion | flops 150994944 | bytes 4128772 | tf_op jit(solution)/shard_map/cpq,cpn->cqn/dot_general | solution.py:75
  84.5 3.5 %copy.29 = f32[8,256,384]{1,0,2:T(8,128)} copy(f32[8,256,384]{2,1,0:T(8,128)} %fusion.17) | data formatting | bytes 6291456 | tf_op jit(solution)/shard_map/cpq,cpn->cqn/dot_general | solution.py:75
  88.0 2.2 slice.30
  90.2 1.9 collective-permute-start
  92.1 3.3 %fusion.15 = f32[8,256,384]{2,1,0:T(8,128)} fusion(bf16[8,3,96,384]{3,2,1,0:T(8,128)(2,1)} %param.15, bf16[8,384,256]{2,1,0:T(8,128)(2,1)S(1)} %copy-done, s32[]{:T(128)S(6)} %select_n.27), kind=kOutput, calls=%fused_computation.17 | convolution fusion | flops 150994944 | bytes 4128772 | tf_op jit(solution)/shard_map/cpq,cpn->cqn/dot_general | solution.py:75
  95.5 3.6 %copy.31 = f32[8,256,384]{1,0,2:T(8,128)} copy(f32[8,256,384]{2,1,0:T(8,128)} %fusion.15) | data formatting | bytes 6291456 | tf_op jit(solution)/shard_map/cpq,cpn->cqn/dot_general | solution.py:75
  99.1 2.8 %slice.33 = f32[1,384,256]{2,0,1:T(1,128)} slice(f32[8,384,256]{2,0,1:T(8,128)} %bitcast.58), slice={[0:1], [0:384], [0:256]} | slice | bytes 786432 | tf_op jit(solution)/shard_map/slice | solution.py:81
  101.9 2.9 %collective-permute-start.1 = (f32[1,384,256]{2,0,1:T(1,128)}, f32[1,384,256]{2,0,1:T(1,128)}, u32[]{:S(2)}, u32[]{:S(2)}) collective-permute-start(f32[1,384,256]{2,0,1:T(1,128)} %slice.33), channel_id=1, source_target_pairs={{0,28},{4,0},{8,4},{12,8},{16,12},{20,16},{24,20},{28,24},{1,29},{... | collective-permute-start | bytes 1179656 | tf_op jit(solution)/shard_map/ppermute | solution.py:10
  104.8 3.8 %slice.32 = f32[7,384,256]{2,0,1:T(8,128)} slice(f32[8,384,256]{2,0,1:T(8,128)} %bitcast.59), slice={[1:8], [0:384], [0:256]} | slice | bytes 5505024 | tf_op jit(solution)/shard_map/slice | solution.py:86
  108.7 3.4 %fusion.19 = f32[8,256,384]{2,1,0:T(8,128)} fusion(bf16[8,3,96,384]{3,2,1,0:T(8,128)(2,1)} %param.15, bf16[8,384,256]{2,1,0:T(8,128)(2,1)S(1)} %copy-done, s32[]{:T(128)S(6)} %select_n.27), kind=kOutput, calls=%fused_computation.21 | convolution fusion | flops 150994944 | bytes 4128772 | tf_op jit(solution)/shard_map/cpq,cpn->cqn/dot_general | solution.py:75
  112.0 3.6 %copy.27 = f32[8,256,384]{1,0,2:T(8,128)} copy(f32[8,256,384]{2,1,0:T(8,128)} %fusion.19) | data formatting | bytes 6291456 | tf_op jit(solution)/shard_map/cpq,cpn->cqn/dot_general | solution.py:75
  116.9 19.4 %all-to-all-done.1 = bf16[8,6,384,64]{2,3,1,0:T(8,128)(2,1)} async-done(((bf16[8,6,384,64]{2,3,1,0:T(8,128)(2,1)}), bf16[8,6,384,64]{2,3,1,0:T(8,128)(2,1)}, u32[]{:S(2)}, u32[]{:S(2)}) %all-to-all-start.1) | async-done | bytes 2359328 | tf_op jit(solution)/shard_map/all_to_all | solution.py:48
  136.3 4.5 %convolution_convert_fusion = bf16[8,6,384,256]{3,2,1,0:T(8,128)(2,1)S(1)} fusion(bf16[8,6,384,64]{2,3,1,0:T(8,128)(2,1)} %all-to-all-done.1, bf16[8,6,64,256]{3,2,1,0:T(8,128)(2,1)S(1)} %all-to-all-done.2), kind=kOutput, calls=%fused_computation.7 | convolution fusion | flops 608698368 | bytes 13369344 | tf_op jit(solution)/shard_map/smcr,smrn->smcn/dot_general | solution.py:46
  140.8 9.6 %fusion.6 = f32[8,384,256]{2,0,1:T(8,128)} fusion(f32[7,384,256]{2,0,1:T(8,128)S(1)} %bitcast.57, f32[1,384,256]{2,0,1:T(1,128)} %collective-permute-done, f32[1,384,256]{2,0,1:T(1,128)} %collective-permute-done.1, f32[7,384,256]{2,0,1:T(8,128)} %slice.32, f32[8,256,384]{1,0,2:T(8,128)} %copy.27, s32[48]{0:T(128)S(1)} %eq.35, ...), kind=kOutput, calls=%fused_computation.12 | convolution fusion | flops 79430016 | bytes 22020288 | tf_op jit(solution)/shard_map/dot_general | solution.py:68
  150.4 74.2 %all-reduce.2.cloned.1.call-done = f32[8,384,256]{2,0,1:T(8,128)} async-done(((f32[8,384,256]{2,0,1:T(8,128)}), f32[8,384,256]{2,0,1:T(8,128)}) %all-reduce.2.cloned.1.call-update) | async-done | bytes 3145744 | tf_op jit(solution)/shard_map/psum | solution.py:88
  224.5 4.6 %copy.32 = f32[8,384,256]{2,1,0:T(8,128)} copy(f32[8,384,256]{2,0,1:T(8,128)} %all-reduce.2.cloned.1.call-done) | data formatting | bytes 6291456 | tf_op jit(solution)/shard_map/psum | solution.py:88
  (16 shorter events, 2.6 us)
Async XLA Ops:
  6.5 13.3 %copy-start = (bf16[8,384,256]{2,1,0:T(8,128)(2,1)S(1)}, bf16[8,384,256]{2,1,0:T(8,128)(2,1)}, u32[]{:S(2)}) copy-start(bf16[8,384,256]{2,1,0:T(8,128)(2,1)} %param.8) | copy-start | bytes 4718596
  10.4 23.8 %all-to-all-start = ((s32[8,1,6]{2,1,0:T(1,128)}), s32[8,1,6]{2,1,0:T(1,128)S(1)}, u32[]{:S(2)}, u32[]{:S(2)}) async-start(s32[8,1,6]{2,1,0:T(1,128)} %bitcast.3), calls=%async_computation | async-start | bytes 8192 | tf_op jit(solution)/shard_map/all_to_all | solution.py:37
  34.2 42.4 %all-to-all-start.2 = ((bf16[8,6,64,256]{3,2,1,0:T(8,128)(2,1)}), bf16[8,6,64,256]{3,2,1,0:T(8,128)(2,1)S(1)}, u32[]{:S(2)}, u32[]{:S(2)}) async-start(bf16[8,6,64,256]{3,2,1,0:T(8,128)(2,1)} %bitcast.7), calls=%async_computation.2 | async-start | bytes 3145728 | tf_op jit(solution)/shard_map/all_to_all | solution.py:55
  76.7 59.6 %all-to-all-start.1 = ((bf16[8,6,384,64]{2,3,1,0:T(8,128)(2,1)}), bf16[8,6,384,64]{2,3,1,0:T(8,128)(2,1)}, u32[]{:S(2)}, u32[]{:S(2)}) async-start(bf16[8,6,384,64]{2,3,1,0:T(8,128)(2,1)} %bitcast.55), calls=%async_computation.1 | async-start | bytes 4718592 | tf_op jit(solution)/shard_map/all_to_all | solution.py:48
  81.1 143.5 %all-reduce.2.cloned.1.call-start = ((), (), s32[]{:S(2)}) async-start(), calls=%async_computation.3 | async-start | bytes 6291456 | tf_op jit(solution)/shard_map/psum | solution.py:88
  90.2 50.5 %collective-permute-start = (f32[1,384,256]{2,0,1:T(1,128)S(1)}, f32[1,384,256]{2,0,1:T(1,128)}, u32[]{:S(2)}, u32[]{:S(2)}) collective-permute-start(f32[1,384,256]{2,0,1:T(1,128)S(1)} %slice.30), channel_id=1, source_target_pairs={{0,4},{4,8},{8,12},{12,16},{16,20},{20,24},{24,28},{28,0},{1,5},{5... | collective-permute-start | bytes 1179656 | tf_op jit(solution)/shard_map/ppermute | solution.py:10
  101.9 38.8 %collective-permute-start.1 = (f32[1,384,256]{2,0,1:T(1,128)}, f32[1,384,256]{2,0,1:T(1,128)}, u32[]{:S(2)}, u32[]{:S(2)}) collective-permute-start(f32[1,384,256]{2,0,1:T(1,128)} %slice.33), channel_id=1, source_target_pairs={{0,28},{4,0},{8,4},{12,8},{16,12},{20,16},{24,20},{28,24},{1,29},{... | collective-permute-start | bytes 1179656 | tf_op jit(solution)/shard_map/ppermute | solution.py:10
  136.3 4.5 %copy-start.1 = (f32[8,256,384]{1,0,2:T(8,128)S(1)}, f32[8,256,384]{1,0,2:T(8,128)}, u32[]{:S(2)}) copy-start(f32[8,256,384]{1,0,2:T(8,128)} %copy.29) | copy-start | bytes 9437188
Sparse Core Ops, SparseCore 0:
  150.5 73.9 all-reduce.1
where the time goes:
time: 237 us; the launch traced here: 236 us
  waiting for transfers between devices  122 us (51%)
  local copies, waits for them, and re-layouts  43.5 us (18%)
  matrix products  29 us (12%)
  starting transfers between devices  22.5 us (9%)
  between operations  13.5 us (6%)
  other arithmetic  5.04 us (2%)
    psum x1, waiting for transfers between devices, shards(): return lax.psum(total_here, 'rep')  74.2 us
    all_to_all x1, waiting for transfers between devices, shards(): lax.all_to_all(packed_coeffs.reshape(owners, most_slots, rank_pad, column...  28.8 us
    all_to_all x1, waiting for transfers between devices, shards(): lax.all_to_all(packed_right.reshape(owners, most_slots, width, rank_pad),...  19.4 us
    dot_general x3, local copies, waits for them, and re-layouts, shards(): jnp.einsum('cpq,cpn->cqn', near_blocks[:, offset], local_rows, preferred_...  10.8 us
    dot_general x3, matrix products, shards(): jnp.einsum('cpq,cpn->cqn', near_blocks[:, offset], local_rows, preferred_...  10.1 us
    dot_general x1, matrix products, shards(): jnp.dot(chooser, flattened, preferred_element_type=jnp.float32)  9.55 us
    all_to_all x1, starting transfers between devices, shards(): lax.all_to_all(labels.reshape(owners, most_slots), 'rows', split_axis=0,...  7.31 us
    all_to_all x1, starting transfers between devices, shards(): lax.all_to_all(packed_coeffs.reshape(owners, most_slots, rank_pad, column...  6 us
  transfers between devices with their start and end apart: 6, of which 3 were waited for; matrix products, arithmetic and copies ran while one was open for 25% of the time, Pallas kernels for 0%

commit v1 on v0

v1 whole, which is shorter than its diff:
```python
import functools

import jax
import jax.numpy as jnp
from jax import lax
from jax.experimental import pallas as pl
from jax.experimental.pallas import tpu as pltpu
from jax.sharding import PartitionSpec as P

MESH = pl.DeviceIdType.MESH
PARTS = 2
BF16 = jnp.bfloat16
F32 = jnp.float32


def dot_rows(left, right):
    return lax.dot_general(left, right, (((0,), (0,)), ((), ())), preferred_element_type=F32)


def kernel(
    owners, reps, most, tab, field, ut, vt, near, out,
    vsend, vrecv, vtr, csend, crecv, hnear, hfield, total, *rest,
):
    stages = reps.bit_length() - 1
    rsend, rrecv = rest[:stages], rest[stages:2 * stages]
    vs, vr, cs, cr, hs, hr, rs, rr, gs, gr = rest[2 * stages:]
    row, rep = lax.axis_index("rows"), lax.axis_index("rep")
    blocks, rank, width = ut.shape
    clusters, _, columns = field.shape
    share = near.shape[2]
    part = columns // PARTS
    depth = most * rank
    peers = owners - 1

    barrier = pltpu.get_barrier_semaphore()

    @pl.loop(1, owners)
    def _(d):
        pl.semaphore_signal(
            barrier, inc=1, device_id=(lax.rem(row + d, owners), rep), device_id_type=MESH
        )

    @pl.loop(1, reps)
    def _(d):
        pl.semaphore_signal(
            barrier, inc=1, device_id=(row, lax.rem(rep + d, reps)), device_id_type=MESH
        )

    def turn(k):
        step = (k + 1) // 2
        return owners // 2 + lax.rem(k, 2) * step - (1 - lax.rem(k, 2)) * step

    def v_copy(d):
        return pltpu.make_async_remote_copy(
            src_ref=vsend.at[d], dst_ref=vrecv.at[d], send_sem=vs.at[d], recv_sem=vr.at[d],
            device_id=(lax.rem(row + d, owners), rep), device_id_type=MESH,
        )

    def c_copy(h, d):
        return pltpu.make_async_remote_copy(
            src_ref=csend.at[h, d], dst_ref=crecv.at[h, d],
            send_sem=cs.at[h, d], recv_sem=cr.at[h, d],
            device_id=(lax.rem(row + d, owners), rep), device_id_type=MESH,
        )

    def pack(d, target):
        owner = lax.rem(row + d, owners)
        for j in range(most):
            target[d, pl.ds(j * rank, rank), :] = vt[tab[0, owner * most + j]]

    def coeffs(d, target):
        owner = lax.rem(row + d, owners)
        extra = csend.shape[2] - depth
        lines = lax.broadcasted_iota(jnp.int32, (extra, part), 0)
        marks = jnp.full((extra, part), clusters, jnp.int32)
        for j in range(most):
            slot = owner * most + j
            value = jnp.dot(ut[tab[0, slot]], field[tab[1, slot]], preferred_element_type=F32)
            kept = lax.broadcasted_iota(jnp.int32, (rank, columns), 0) < tab[2, slot]
            value = jnp.where(kept, value, 0.0).astype(BF16)
            for h in range(PARTS):
                target[h, d, pl.ds(j * rank, rank), :] = value[:, h * part:(h + 1) * part]
            marks = jnp.where(lines == j, tab[3, slot], marks)
        for h in range(PARTS):
            target[h, d, pl.ds(depth, extra), :] = marks.astype(F32).astype(BF16)

    my_rows = pl.ds(pl.multiple_of(rep * share, share), share)

    def halo_copies():
        made = []
        for side, cluster, offset, shift in ((0, clusters - 1, 2, 1), (1, 0, 0, owners - 1)):
            where = (lax.rem(row + shift, owners), rep)
            made.append(pltpu.make_async_remote_copy(
                src_ref=near.at[cluster, offset], dst_ref=hnear.at[side],
                send_sem=hs.at[2 * side], recv_sem=hr.at[2 * side],
                device_id=where, device_id_type=MESH,
            ))
            made.append(pltpu.make_async_remote_copy(
                src_ref=field.at[cluster, my_rows, :], dst_ref=hfield.at[side],
                send_sem=hs.at[2 * side + 1], recv_sem=hr.at[2 * side + 1],
                device_id=where, device_id_type=MESH,
            ))
        return made

    pl.semaphore_wait(barrier, owners + reps - 2)

    @pl.loop(0, peers)
    def _(k):
        d = turn(k)
        pack(d, vsend)
        v_copy(d).start()

    halos = halo_copies()
    for copy in halos:
        copy.start()

    @pl.loop(0, peers)
    def _(k):
        d = turn(k)
        coeffs(d, csend)
        c_copy(0, d).start()

    for h in range(1, PARTS):
        @pl.loop(0, peers)
        def _(k):
            c_copy(h, turn(k)).start()

    pack(0, vrecv)
    coeffs(0, crecv)

    def put(c, value):
        for h in range(PARTS):
            total[h, c] = value[:, h * part:(h + 1) * part]

    def add(c, value):
        for h in range(PARTS):
            total[h, c] = total[h, c] + value[:, h * part:(h + 1) * part]

    @pl.loop(0, clusters)
    def _(c):
        put(c, dot_rows(near[c, 1], field[c, my_rows, :]))

    @pl.loop(0, clusters - 1)
    def _(c):
        add(c + 1, dot_rows(near[c, 2], field[c, my_rows, :]))
        add(c, dot_rows(near[c + 1, 0], field[c + 1, my_rows, :]))

    for copy in halos:
        copy.wait_recv()
    add(0, dot_rows(hnear[0], hfield[0]))
    add(clusters - 1, dot_rows(hnear[1], hfield[1]))

    def far(h, d):
        if h == 0:
            vtr[d] = vrecv[d].T
        labels = jnp.concatenate(
            [
                jnp.broadcast_to(crecv[h, d, pl.ds(depth + j, 1), :].astype(F32), (rank, part))
                for j in range(most)
            ],
            axis=0,
        ).astype(BF16)

        @pl.loop(0, clusters)
        def _(c):
            chosen = labels == c.astype(F32).astype(BF16)
            picked = jnp.where(chosen, crecv[h, d, pl.ds(0, depth), :], jnp.zeros((), BF16))
            total[h, c] = total[h, c] + jnp.dot(vtr[d], picked, preferred_element_type=F32)

    def far_span(h, first, last):
        @pl.loop(first, last)
        def _(k):
            d = turn(peers - 1 - k)
            if h == 0:
                v_copy(d).wait_recv()
            c_copy(h, d).wait_recv()
            far(h, d)

    plan = []
    low, size = 0, clusters
    for t in range(stages):
        bit = lax.rem(rep // (1 << t), 2)
        half = size // 2
        partner = rep + (1 << t) * (1 - 2 * bit)
        plan.append((half, partner, low + bit * half, low + (1 - bit) * half))
        low, size = low + bit * half, half

    def r_copy(h, t):
        return pltpu.make_async_remote_copy(
            src_ref=rsend[t].at[h], dst_ref=rrecv[t].at[h],
            send_sem=rs.at[h, t], recv_sem=rr.at[h, t],
            device_id=(row, plan[t][1]), device_id_type=MESH,
        )

    def g_copy(h, t):
        half, partner, keep, _ = plan[t]
        block = out.at[pl.ds(keep, half), :, pl.ds(h * part, part)]
        return pltpu.make_async_remote_copy(
            src_ref=block, dst_ref=block, send_sem=gs.at[h, t], recv_sem=gr.at[h, t],
            device_id=(row, partner), device_id_type=MESH,
        )

    def give(h, t):
        half, _, _, away = plan[t]

        @pl.loop(0, half)
        def _(i):
            rsend[t][h, i] = total[h, away + i].astype(BF16)

        r_copy(h, t).start()

    def take(h, t):
        half, _, keep, _ = plan[t]
        r_copy(h, t).wait_recv()

        @pl.loop(0, half)
        def _(i):
            value = total[h, keep + i] + rrecv[t][h, i].astype(F32)
            if t == stages - 1:
                out[keep + i, :, pl.ds(h * part, part)] = value.astype(BF16)
            else:
                total[h, keep + i] = value

    def sequence(h):
        steps = [lambda: give(h, 0)]
        for t in range(stages):
            if t < stages - 1:
                steps.append(lambda t=t: (take(h, t), give(h, t + 1)))
            else:
                steps.append(lambda t=t: (take(h, t), g_copy(h, t).start()))
        for t in range(stages - 1, 0, -1):
            steps.append(lambda t=t: (g_copy(h, t).wait_recv(), g_copy(h, t - 1).start()))
        steps.append(lambda: g_copy(h, 0).wait_recv())
        return steps

    ahead, behind = sequence(0), sequence(1)
    far(0, 0)
    far_span(0, 0, peers)
    ahead[0]()
    for step in ahead[1:stages]:
        step()
    middle = peers // 2
    far(1, 0)
    far_span(1, 0, middle)
    ahead[stages]()
    far_span(1, middle, peers)
    behind[0]()
    later = ahead[stages + 1:]
    for place, step in enumerate(behind[1:]):
        if place < len(later):
            later[place]()
        step()

    @pl.loop(1, owners)
    def _(d):
        v_copy(d).wait_send()
        for h in range(PARTS):
            c_copy(h, d).wait_send()

    for copy in halos:
        copy.wait_send()
    for h in range(PARTS):
        for t in range(stages):
            r_copy(h, t).wait_send()
            g_copy(h, t).wait_send()


def shards(
    field_in,
    left_factors,
    right_factors,
    block_ranks,
    row_cluster,
    col_owner,
    col_cluster,
    near_blocks,
):
    owners, reps = lax.axis_size("rows"), lax.axis_size("rep")
    blocks, width, rank = left_factors.shape
    clusters, _, columns = field_in.shape
    share = near_blocks.shape[2]
    most = 5 * blocks // (4 * owners) + 1
    part = columns // PARTS
    depth = most * rank
    tall = depth + -(-most // 16) * 16
    stages = reps.bit_length() - 1

    target = col_owner[:, 0]
    number = jnp.arange(blocks, dtype=jnp.int32)
    same = (target[:, None] == target[None, :]) & (number[None, :] < number[:, None])
    slot = target * most + jnp.sum(same.astype(jnp.int32), axis=1)
    held = slot[:, None] == jnp.arange(owners * most, dtype=jnp.int32)[None, :]
    facts = jnp.stack([number, row_cluster, block_ranks, col_cluster - clusters])
    tab = jnp.sum(jnp.where(held[None], facts[:, :, None], 0), axis=1)
    tab = tab + jnp.array([0, 0, 0, clusters], jnp.int32)[:, None]

    vmem = pl.BlockSpec(memory_space=pltpu.VMEM)
    dma = pltpu.SemaphoreType.DMA
    halves = [clusters >> (t + 1) for t in range(stages)]
    steps = [pltpu.VMEM((PARTS, half, width, part), BF16) for half in halves]
    gathered = pl.pallas_call(
        functools.partial(kernel, owners, reps, most),
        out_shape=jax.ShapeDtypeStruct(field_in.shape, BF16),
        in_specs=[pl.BlockSpec(memory_space=pltpu.SMEM)] + [vmem] * 4,
        out_specs=vmem,
        scratch_shapes=[
            pltpu.VMEM((owners, depth, width), BF16),
            pltpu.VMEM((owners, depth, width), BF16),
            pltpu.VMEM((owners, width, depth), BF16),
            pltpu.VMEM((PARTS, owners, tall, part), BF16),
            pltpu.VMEM((PARTS, owners, tall, part), BF16),
            pltpu.VMEM((2, share, width), BF16),
            pltpu.VMEM((2, share, columns), BF16),
            pltpu.VMEM((PARTS, clusters, width, part), F32),
            *steps,
            *steps,
            dma((owners,)),
            dma((owners,)),
            dma((PARTS, owners)),
            dma((PARTS, owners)),
            dma((4,)),
            dma((4,)),
            dma((PARTS, stages)),
            dma((PARTS, stages)),
            dma((PARTS, stages)),
            dma((PARTS, stages)),
        ],
        compiler_params=pltpu.CompilerParams(
            collective_id=0, has_side_effects=True, vmem_limit_bytes=60 * 1024 * 1024
        ),
    )(
        tab,
        field_in,
        jnp.swapaxes(left_factors, 1, 2),
        jnp.swapaxes(right_factors, 1, 2),
        near_blocks,
    )
    return gathered.astype(F32)


def solution(mesh):
    in_specs = (
        P("rows", None, None),
        P(("rows", "rep"), None, None),
        P(("rows", "rep"), None, None),
        P(("rows", "rep")),
        P(("rows", "rep")),
        P(("rows", "rep"), None),
        P(("rows", "rep")),
        P("rows", None, "rep", None),
    )
    out_specs = P("rows", None, None)
    return jax.shard_map(shards, mesh=mesh, in_specs=in_specs, out_specs=out_specs, check_vma=False)
```

time: 237 us -> 144 us (0.61)
  the two profiles are of different devices: /device:TPU:0 before, /device:TPU:19 now
where the time goes in v1:
time: 144 us
  Pallas kernels  136 us (94%)
  other arithmetic  7.74 us (5%)
    pallas_call x1, Pallas kernels, shards(): pl.pallas_call(functools.partial(kernel, owners, reps, most), out_shape=j...  136 us
    convert_element_type x1, other arithmetic, shards(): return gathered.astype(F32)  3.36 us

profile of v1, /device:TPU:19, one launch (start us, length us, event | category | flops | bytes accessed | tf_op | source)
XLA Modules:
  0.0 143.5 jit_solution(12426420724756636212)
XLA Ops:
  0.0 0.7 add_bitcast_fusion
  0.7 0.9 convert_reduce_fusion
  1.6 0.7 fusion.1
  2.2 0.7 pad_add_fusion
  2.9 0.1 iota_compare_fusion
  3.0 0.1 select_reduce_fusion
  3.1 1.3 broadcast_add_fusion.tab
  4.4 135.8 %shard_map.91 = bf16[8,384,256]{2,1,0:T(8,128)(2,1)} custom-call(s32[4,48]{1,0:T(4,128)} %broadcast_add_fusion.tab, bf16[8,384,256]{2,1,0:T(8,128)(2,1)} %field.1, bf16[32,64,384]{2,1,0:T(8,128)(2,1)} %bitcast.13, bf16[32,64,384]{2,1,0:T(8,128)(2,1)} %bitcast.14, bf16[8,3,96,384]{3,2,1,0:T(8,128)(2,1)} %near.1), custom_call_target="tpu_custom_call" | custom-call | tf_op jit(solution)/shard_map/pallas_call | solution.py:301
  140.2 3.4 %convert_element_type.7 = f32[8,384,256]{2,1,0:T(8,128)} convert(bf16[8,384,256]{2,1,0:T(8,128)(2,1)} %shard_map.91) | non-fusion elementwise | flops 786432 | bytes 4718592 | tf_op jit(solution)/shard_map/convert_element_type | solution.py:338
  (1 shorter events, 0.0 us)

commit v2 on v1

--- a/solution.py
+++ b/solution.py
@@ -18,19 +18,23 @@
 
 
 def kernel(
-    owners, reps, most, tab, field, ut, vt, near, out,
+    owners, reps, most, joint, tab, field, ut, vt, near, out,
     vsend, vrecv, vtr, csend, crecv, hnear, hfield, total, *rest,
 ):
     stages = reps.bit_length() - 1
     rsend, rrecv = rest[:stages], rest[stages:2 * stages]
-    vs, vr, cs, cr, hs, hr, rs, rr, gs, gr = rest[2 * stages:]
+    vs, vr, cs, cr, hs, hr, rs, rr, gs, gr = rest[2 * stages:2 * stages + 10]
+    extras = rest[2 * stages + 10:]
+    group = owners // 2 if joint else owners
     row, rep = lax.axis_index("rows"), lax.axis_index("rep")
+    place_in = lax.rem(row, group)
+    base = row - place_in
     blocks, rank, width = ut.shape
     clusters, _, columns = field.shape
     share = near.shape[2]
     part = columns // PARTS
     depth = most * rank
-    peers = owners - 1
+    peers = group - 1
 
     barrier = pltpu.get_barrier_semaphore()
 
@@ -46,30 +50,31 @@
             barrier, inc=1, device_id=(row, lax.rem(rep + d, reps)), device_id_type=MESH
         )
 
+    def peer(d):
+        return base + lax.rem(place_in + d, group)
+
     def turn(k):
         step = (k + 1) // 2
-        return owners // 2 + lax.rem(k, 2) * step - (1 - lax.rem(k, 2)) * step
+        return group // 2 + lax.rem(k, 2) * step - (1 - lax.rem(k, 2)) * step
 
     def v_copy(d):
         return pltpu.make_async_remote_copy(
             src_ref=vsend.at[d], dst_ref=vrecv.at[d], send_sem=vs.at[d], recv_sem=vr.at[d],
-            device_id=(lax.rem(row + d, owners), rep), device_id_type=MESH,
+            device_id=(peer(d), rep), device_id_type=MESH,
         )
 
     def c_copy(h, d):
         return pltpu.make_async_remote_copy(
             src_ref=csend.at[h, d], dst_ref=crecv.at[h, d],
             send_sem=cs.at[h, d], recv_sem=cr.at[h, d],
-            device_id=(lax.rem(row + d, owners), rep), device_id_type=MESH,
-        )
-
-    def pack(d, target):
-        owner = lax.rem(row + d, owners)
+            device_id=(peer(d), rep), device_id_type=MESH,
+        )
+
+    def pack(d, target, owner):
         for j in range(most):
             target[d, pl.ds(j * rank, rank), :] = vt[tab[0, owner * most + j]]
 
-    def coeffs(d, target):
-        owner = lax.rem(row + d, owners)
+    def coeffs(d, target, owner):
         extra = csend.shape[2] - depth
         lines = lax.broadcasted_iota(jnp.int32, (extra, part), 0)
         marks = jnp.full((extra, part), clusters, jnp.int32)
@@ -102,12 +107,155 @@
             ))
         return made
 
+    plan = []
+    low, size = 0, clusters
+    for t in range(stages):
+        bit = lax.rem(rep // (1 << t), 2)
+        half = size // 2
+        partner = rep + (1 << t) * (1 - 2 * bit)
+        plan.append((half, partner, low + bit * half, low + (1 - bit) * half))
+        low, size = low + bit * half, half
+
+    def labels_of(source, h, d):
+        return jnp.concatenate(
+            [
+                jnp.broadcast_to(source[h, d, pl.ds(depth + j, 1), :].astype(F32), (rank, part))
+                for j in range(most)
+            ],
+            axis=0,
+        ).astype(BF16)
+
+    def part_of(right, source, labels, h, d, c):
+        label = jnp.asarray(c, jnp.int32).astype(F32).astype(BF16)
+        picked = jnp.where(
+            labels == label, source[h, d, pl.ds(0, depth), :], jnp.zeros((), BF16)
+        )
+        return jnp.dot(right[d], picked, preferred_element_type=F32)
+
+    levels = []
+    crossed = None
+    if joint:
+        count = stages + group.bit_length() - 1
+        jsend, jrecv = extras[:count], extras[count:2 * count]
+        fv, fvt, fc, ftot, xsend, xrecv, js, jr, xs, xr = extras[2 * count:]
+        crossed = xrecv
+        first = plan[0][2]
+        away_base = owners // 2 - base
+        for h in range(PARTS):
+            kinds = [("c", t) for t in range(stages)]
+            kinds += [("e", g) for g in range(group.bit_length() - 1)]
+            if h % 2:
+                kinds = [kinds[0], kinds[stages], *kinds[1:stages], *kinds[stages + 1:]]
+            mine, free = 0, list(range(group.bit_length() - 1))
+            start, size = 0, clusters
+            rows = []
+            for kind, t in kinds:
+                if kind == "c":
+                    half, partner, keep, away = plan[t]
+                    who = (row, partner)
+                    size = half
+                    keep_at, away_at = (keep, half), (away, half)
+                    start = keep
+                    keep_es = away_es = (mine, list(free))
+                else:
+                    bit = lax.rem(place_in // (1 << t), 2)
+                    who = (row + (1 << t) * (1 - 2 * bit), rep)
+                    free.remove(t)
+                    keep_es = (mine + bit * (1 << t), list(free))
+                    away_es = (mine + (1 - bit) * (1 << t), list(free))
+                    mine = keep_es[0]
+                    keep_at = away_at = (start, size)
+                rows.append((who, keep_es, keep_at, away_es, away_at))
+            levels.append(rows)
+
+    def each(es, span, body):
+        offset, free = es
+        combos = [0]
+        for bit in free:
+            combos = combos + [value + (1 << bit) for value in combos]
+        for spot, combo in enumerate(combos):
+            @pl.loop(0, span[1])
+            def _(i):
+                body(spot * span[1] + i, offset + combo, span[0] + i)
+
+    def j_copy(h, t):
+        return pltpu.make_async_remote_copy(
+            src_ref=jsend[t].at[h], dst_ref=jrecv[t].at[h],
+            send_sem=js.at[h, t], recv_sem=jr.at[h, t],
+            device_id=levels[h][t][0], device_id_type=MESH,
+        )
+
+    def x_copy(h):
+        return pltpu.make_async_remote_copy(
+            src_ref=xsend.at[h], dst_ref=xrecv.at[h],
+            send_sem=xs.at[h], recv_sem=xr.at[h],
+            device_id=(away_base + place_in, rep), device_id_type=MESH,
+        )
+
+    def j_give(h, t):
+        _, _, _, es, span = levels[h][t]
+
+        def body(n, e, c):
+            jsend[t][h, n] = ftot[h, e, c - first].astype(BF16)
+
+        each(es, span, body)
+        j_copy(h, t).start()
+
+    def j_take(h, t):
+        _, es, span, _, _ = levels[h][t]
+        j_copy(h, t).wait_recv()
+
+        def body(n, e, c):
+            ftot[h, e, c - first] = ftot[h, e, c - first] + jrecv[t][h, n].astype(F32)
+
+        each(es, span, body)
+
+    def j_first(h):
+        half, _, keep, away = plan[0]
+
+        @pl.loop(0, group)
+        def _(e):
+            labels = labels_of(fc, h, e)
+
+            @pl.loop(0, half)
+            def _(i):
+                jsend[0][h, e * half + i] = part_of(fvt, fc, labels, h, e, away + i).astype(BF16)
+
+        j_copy(h, 0).start()
+
+        @pl.loop(0, group)
+        def _(e):
+            labels = labels_of(fc, h, e)
+
+            @pl.loop(0, half)
+            def _(i):
+                ftot[h, e, i] = part_of(fvt, fc, labels, h, e, keep + i)
+
+    def j_last(h):
+        j_take(h, count - 1)
+
+        @pl.loop(0, plan[-1][0])
+        def _(i):
+            xsend[h, i] = ftot[h, place_in, plan[-1][2] + i - first].astype(BF16)
+
+        x_copy(h).start()
+
     pl.semaphore_wait(barrier, owners + reps - 2)
+
+    if joint:
+        @pl.loop(0, group)
+        def _(e):
+            pack(e, fv, away_base + e)
+            coeffs(e, fc, away_base + e)
+            fvt[e] = fv[e].T
+
+        for h in range(PARTS):
+            j_first(h)
 
     @pl.loop(0, peers)
     def _(k):
         d = turn(k)
-        pack(d, vsend)
+        pack(d, vsend, peer(d))
         v_copy(d).start()
 
     halos = halo_copies()
@@ -117,7 +265,7 @@
     @pl.loop(0, peers)
     def _(k):
         d = turn(k)
-        coeffs(d, csend)
+        coeffs(d, csend, peer(d))
         c_copy(0, d).start()
 
     for h in range(1, PARTS):
@@ -125,8 +273,13 @@
         def _(k):
             c_copy(h, turn(k)).start()
 
-    pack(0, vrecv)
-    coeffs(0, crecv)
+    if joint:
+        for h in range(PARTS):
+            j_take(h, 0)
+            j_give(h, 1)
+
+    pack(0, vrecv, row)
+    coeffs(0, crecv, row)
 
     def put(c, value):
         for h in range(PARTS):
@@ -153,19 +306,11 @@
     def far(h, d):
         if h == 0:
             vtr[d] = vrecv[d].T
-        labels = jnp.concatenate(
-            [
-                jnp.broadcast_to(crecv[h, d, pl.ds(depth + j, 1), :].astype(F32), (rank, part))
-                for j in range(most)
-            ],
-            axis=0,
-        ).astype(BF16)
+        labels = labels_of(crecv, h, d)
 
         @pl.loop(0, clusters)
         def _(c):
-            chosen = labels == c.astype(F32).astype(BF16)
-            picked = jnp.where(chosen, crecv[h, d, pl.ds(0, depth), :], jnp.zeros((), BF16))
-            total[h, c] = total[h, c] + jnp.dot(vtr[d], picked, preferred_element_type=F32)
+            total[h, c] = total[h, c] + part_of(vtr, crecv, labels, h, d, c)
 
     def far_span(h, first, last):
         @pl.loop(first, last)
@@ -176,15 +321,6 @@
             c_copy(h, d).wait_recv()
             far(h, d)
 
-    plan = []
-    low, size = 0, clusters
-    for t in range(stages):
-        bit = lax.rem(rep // (1 << t), 2)
-        half = size // 2
-        partner = rep + (1 << t) * (1 - 2 * bit)
-        plan.append((half, partner, low + bit * half, low + (1 - bit) * half))
-        low, size = low + bit * half, half
-
     def r_copy(h, t):
         return pltpu.make_async_remote_copy(
             src_ref=rsend[t].at[h], dst_ref=rrecv[t].at[h],
@@ -205,7 +341,7 @@
 
         @pl.loop(0, half)
         def _(i):
-            rsend[t][h, i] = total[h, away + i].astype(BF16)
+            rsend[t][h, i] = total[h, away + i].astype(rsend[t].dtype)
 
         r_copy(h, t).start()
 
@@ -217,6 +353,8 @@
         def _(i):
             value = total[h, keep + i] + rrecv[t][h, i].astype(F32)
             if t == stages - 1:
+                if joint:
+                    value = value + crossed[h, i].astype(F32)
                 out[keep + i, :, pl.ds(h * part, part)] = value.astype(BF16)
             else:
                 total[h, keep + i] = value
@@ -239,23 +377,47 @@
     ahead[0]()
     for step in ahead[1:stages]:
         step()
-    middle = peers // 2
-    far(1, 0)
-    far_span(1, 0, middle)
-    ahead[stages]()
-    far_span(1, middle, peers)
-    behind[0]()
-    later = ahead[stages + 1:]
-    for place, step in enumerate(behind[1:]):
-        if place < len(later):
-            later[place]()
-        step()
-
-    @pl.loop(1, owners)
+    if joint:
+        far(1, 0)
+        far_span(1, 0, peers)
+        for step in behind[:stages]:
+            step()
+        for t in range(1, count - 1):
+            for h in range(PARTS):
+                j_take(h, t)
+                j_give(h, t + 1)
+        for h in range(PARTS):
+            j_last(h)
+        for h in range(PARTS):
+            x_copy(h).wait_recv()
+            (ahead, behind)[h][stages]()
+        for one, two in zip(ahead[stages + 1:], behind[stages + 1:]):
+            one()
+            two()
+    else:
+        middle = peers // 2
+        far(1, 0)
+        far_span(1, 0, middle)
+        ahead[stages]()
+        far_span(1, middle, peers)
+        behind[0]()
+        later = ahead[stages + 1:]
+        for place, step in enumerate(behind[1:]):
+            if place < len(later):
+                later[place]()
+            step()
+
+    @pl.loop(1, group)
     def _(d):
         v_copy(d).wait_send()
         for h in range(PARTS):
             c_copy(h, d).wait_send()
+
+    if joint:
+        for h in range(PARTS):
+            x_copy(h).wait_send()
+            for t in range(count):
+                j_copy(h, t).wait_send()
 
     for copy in halos:
         copy.wait_send()
@@ -297,33 +459,60 @@
     vmem = pl.BlockSpec(memory_space=pltpu.VMEM)
     dma = pltpu.SemaphoreType.DMA
     halves = [clusters >> (t + 1) for t in range(stages)]
-    steps = [pltpu.VMEM((PARTS, half, width, part), BF16) for half in halves]
+    steps = [
+        pltpu.VMEM((PARTS, half, width, part), BF16 if t else F32) for t, half in enumerate(halves)
+    ]
+    joint = owners * clusters * width * columns <= 2 ** 23 and owners >= 4
+    group = owners // 2 if joint else owners
+    more = []
+    if joint:
+        count = stages + group.bit_length() - 1
+        hops = [
+            pltpu.VMEM((PARTS, (group * clusters) >> (t + 1), width, part), BF16)
+            for t in range(count)
+        ]
+        last = pltpu.VMEM((PARTS, halves[-1], width, part), BF16)
+        more = [
+            *hops,
+            *hops,
+            pltpu.VMEM((group, depth, width), BF16),
+            pltpu.VMEM((group, width, depth), BF16),
+            pltpu.VMEM((PARTS, group, tall, part), BF16),
+            pltpu.VMEM((PARTS, group, halves[0], width, part), F32),
+            last,
+            last,
+            dma((PARTS, count)),
+            dma((PARTS, count)),
+            dma((PARTS,)),
+            dma((PARTS,)),
+        ]
     gathered = pl.pallas_call(
-        functools.partial(kernel, owners, reps, most),
+        functools.partial(kernel, owners, reps, most, joint),
         out_shape=jax.ShapeDtypeStruct(field_in.shape, BF16),
         in_specs=[pl.BlockSpec(memory_space=pltpu.SMEM)] + [vmem] * 4,
         out_specs=vmem,
         scratch_shapes=[
-            pltpu.VMEM((owners, depth, width), BF16),
-            pltpu.VMEM((owners, depth, width), BF16),
-            pltpu.VMEM((owners, width, depth), BF16),
-            pltpu.VMEM((PARTS, owners, tall, part), BF16),
-            pltpu.VMEM((PARTS, owners, tall, part), BF16),
+            pltpu.VMEM((group, depth, width), BF16),
+            pltpu.VMEM((group, depth, width), BF16),
+            pltpu.VMEM((group, width, depth), BF16),
+            pltpu.VMEM((PARTS, group, tall, part), BF16),
+            pltpu.VMEM((PARTS, group, tall, part), BF16),
             pltpu.VMEM((2, share, width), BF16),
             pltpu.VMEM((2, share, columns), BF16),
             pltpu.VMEM((PARTS, clusters, width, part), F32),
             *steps,
             *steps,
-            dma((owners,)),
-            dma((owners,)),
-            dma((PARTS, owners)),
-            dma((PARTS, owners)),
+            dma((group,)),
+            dma((group,)),
+            dma((PARTS, group)),
+            dma((PARTS, group)),
             dma((4,)),
             dma((4,)),
             dma((PARTS, stages)),
             dma((PARTS, stages)),
             dma((PARTS, stages)),
             dma((PARTS, stages)),
+            *more,
         ],
         compiler_params=pltpu.CompilerParams(
             collective_id=0, has_side_effects=True, vmem_limit_bytes=60 * 1024 * 1024

time: 144 us -> 121 us (0.84)
  the two profiles are of different devices: /device:TPU:19 before, /device:TPU:0 now
where the time goes in v2:
time: 121 us
  Pallas kernels  113 us (93%)
  other arithmetic  7.74 us (6%)
    pallas_call x1, Pallas kernels, shards(): pl.pallas_call(functools.partial(kernel, owners, reps, most, joint), out_...  113 us
    convert_element_type x1, other arithmetic, shards(): return gathered.astype(F32)  3.36 us

profile of v2, /device:TPU:0, one launch (start us, length us, event | category | flops | bytes accessed | tf_op | source)
XLA Modules:
  0.0 121.0 jit_solution(8086110327415685402)
XLA Ops:
  0.0 0.7 add_bitcast_fusion
  0.7 0.9 convert_reduce_fusion
  1.6 0.7 fusion.1
  2.2 0.7 pad_add_fusion
  2.9 0.1 iota_compare_fusion
  3.0 0.1 select_reduce_fusion
  3.1 1.3 %broadcast_add_fusion.tab = s32[4,48]{1,0:T(4,128)} fusion(s32[4,48]{1,0:T(4,128)S(1)} %select_reduce_fusion, s32[4]{0:T(128)} %constant.9.clone), kind=kLoop, calls=%fused_computation.6 | loop fusion | flops 192 | bytes 1552 | tf_op jit(solution)/shard_map/add | solution.py:457
  4.4 113.2 %shard_map.91 = bf16[8,384,256]{2,1,0:T(8,128)(2,1)} custom-call(s32[4,48]{1,0:T(4,128)} %broadcast_add_fusion.tab, bf16[8,384,256]{2,1,0:T(8,128)(2,1)} %field.1, bf16[32,64,384]{2,1,0:T(8,128)(2,1)} %bitcast.13, bf16[32,64,384]{2,1,0:T(8,128)(2,1)} %bitcast.14, bf16[8,3,96,384]{3,2,1,0:T(8,128)(2,1)} %near.1), custom_call_target="tpu_custom_call" | custom-call | tf_op jit(solution)/shard_map/pallas_call | solution.py:489
  117.6 3.4 %convert_element_type.7 = f32[8,384,256]{2,1,0:T(8,128)} convert(bf16[8,384,256]{2,1,0:T(8,128)(2,1)} %shard_map.91) | non-fusion elementwise | flops 786432 | bytes 4718592 | tf_op jit(solution)/shard_map/convert_element_type | solution.py:527
  (1 shorter events, 0.0 us)
